TPU v7x, 8 devices: a whole 2x2x1 slice. The times are simulated.
8 devices in a mesh: rep: 2 (over y, z), dp: 4 (over x, core).
Axes of the slice: x: 2, y: 2, z: 1, core: 2. Of those that a mesh axis runs over, the one named last changes fastest.
Arguments:
- g_w_gate: bfloat16 [8, 2, 1024, 2816], P(('rep', 'dp')), parts along dimension 0
- g_w_up: bfloat16 [8, 2, 1024, 2816], P(('rep', 'dp')), parts along dimension 0
- g_w_down: bfloat16 [8, 2, 2816, 1024], P(('rep', 'dp')), parts along dimension 0
- w_gate: bfloat16 [2, 1024, 2816], replicated
- w_up: bfloat16 [2, 1024, 2816], replicated
- w_down: bfloat16 [2, 2816, 1024], replicated
- m_w_gate: float32 [2, 1024, 2816], P(None, 'dp')
- m_w_up: float32 [2, 1024, 2816], P(None, 'dp')
- m_w_down: float32 [2, 2816, 1024], P(None, 'dp')
- v_w_gate: float32 [2, 1024, 2816], P(None, 'dp')
- v_w_up: float32 [2, 1024, 2816], P(None, 'dp')
- v_w_down: float32 [2, 2816, 1024], P(None, 'dp')
Outputs:
- output 1: bfloat16 [4, 1024, 2816], P('rep'), parts along dimension 0
- output 2: bfloat16 [4, 1024, 2816], P('rep'), parts along dimension 0
- output 3: bfloat16 [4, 2816, 1024], P('rep'), parts along dimension 0
- output 4: float32 [4, 1024, 2816], P('rep', 'dp'), parts along dimension 0
- output 5: float32 [4, 1024, 2816], P('rep', 'dp'), parts along dimension 0
- output 6: float32 [4, 2816, 1024], P('rep', 'dp'), parts along dimension 0
- output 7: float32 [4, 1024, 2816], P('rep', 'dp'), parts along dimension 0
- output 8: float32 [4, 1024, 2816], P('rep', 'dp'), parts along dimension 0
- output 9: float32 [4, 2816, 1024], P('rep', 'dp'), parts along dimension 0
There are 2 independent parts. A program takes and returns all parts, laid end to end along the dimension named above; an argument that names none is the same for every part.
All inputs are finite; a program needn't handle non-finite values.
Results may differ from a plain program's by a relative error of at most 0.022.
Values are sent between devices in bfloat16 or wider.
A program may use at most 2 GiB of HBM per device.

v0:
```python
import functools

import jax
import jax.numpy as jnp
from jax import lax
from jax.experimental import pallas as pl
from jax.experimental.pallas import tpu as pltpu
from jax.sharding import PartitionSpec as P


LAYERS = 2
SUBS = 4
PER = LAYERS * SUBS
WEIGHTS = 3
GATHERED = 2
CHUNKS = PER * WEIGHTS
SLOTS = 3
AHEAD = 4
PARTS = 4
PIECES = ((0, 1), (2, 3), (4, 5), (6,), (7,))
LATE = GATHERED * PER - 1
ANY = pl.BlockSpec(memory_space=pl.ANY)
VMEM_LIMIT = 60 * 2**20
VMEM_ALL = 67043328
WIDTH = 256


def add_into(dst, at, own, first, rows, cols):
    def body(i, _):
        r = pl.ds(pl.multiple_of(first + i * 16, 16), 16)
        for c in range(0, cols, WIDTH):
            s = pl.ds(c, WIDTH)
            dst[(*at, r, s)] = (dst[(*at, r, s)].astype(jnp.float32) + own[r, s].astype(jnp.float32)).astype(jnp.bfloat16)
        return 0

    lax.fori_loop(0, rows // 16, body, 0)


def step_into(x, at, mine, pair, pair_at, w, m, v, rows, cols):
    def body(i, _):
        r = pl.ds(pl.multiple_of(i * 16, 16), 16)
        for c in range(0, cols, WIDTH):
            s = pl.ds(c, WIDTH)
            g = mine[r, s].astype(jnp.float32) + pair[(*pair_at, r, s)].astype(jnp.float32) + x[(*at, r, s)].astype(jnp.float32)
            g = g.astype(jnp.bfloat16).astype(jnp.float32)
            nm = 0.9 * m[r, s] + 0.1 * g
            nv = 0.95 * v[r, s] + 0.05 * g * g
            old = w[r, s].astype(jnp.float32)
            step = nm * lax.rsqrt(nv + 1e-8) + 0.1 * old
            x[(*at, r, s)] = (old - 0.02 * step).astype(jnp.bfloat16)
            m[r, s] = nm
            v[r, s] = nv
        return 0

    lax.fori_loop(0, rows // 16, body, 0)


def main_kernel(dims, *refs):
    g, w, m, v = (refs[i : i + 3] for i in (0, 3, 6, 9))
    wf, mo, vo = (refs[12 + i : 15 + i] for i in (0, 3, 6))
    pieces, late = refs[21 : 21 + len(PIECES)], refs[21 + len(PIECES)]
    (rv_a, rv_b, xr_a, xr_b, first, ob_a, ob_b, oc_a, oc_b, wc_a, wc_b, mc_a, mc_b, vc_a, vc_b,
     e_s, e_r, x_s, x_r, d_s, d_r, ax_s, ax_r, o_s, o_r, f_s, f_r, lf, lb, lc, st) = refs[22 + len(PIECES) :]
    me = lax.axis_index("dp")
    x, k = me // 2, me % 2
    xo, ko = 1 - x, 1 - k
    partner, across = {"dp": 2 * x + ko}, {"dp": 2 * xo + k}

    def remote(src, dst, s, r, to):
        return pltpu.make_async_remote_copy(src_ref=src, dst_ref=dst, send_sem=s, recv_sem=r, device_id=to, device_id_type=pl.DeviceIdType.MESH)

    class Chunk:
        def __init__(self, c):
            self.c, self.i = c, c // PER
            j = c % PER
            l, sub = j // SUBS, j % SUBS
            a = self.i < 2
            self.slot = slot = c if a else j
            self.rows, self.cols = rows, _ = dims[self.i][0] // SUBS, dims[self.i][1]
            r = pl.ds(sub * rows, rows)
            self.rv, self.xr = (rv_a, xr_a) if a else (rv_b, xr_b)
            self.ob = (ob_a if a else ob_b).at[c % 2]
            p = c % SLOTS
            self.oc, self.wc, self.mc, self.vc = (t.at[p] for t in ((oc_a, wc_a, mc_a, vc_a) if a else (oc_b, wc_b, mc_b, vc_b)))
            gi, wi = g[self.i], wf[self.i]
            n = PARTS if c == 0 else 1
            self.parts = []
            for q in range(n):
                at, size, sem = q * rows // n, rows // n, q if c == 0 else c + PARTS - 1
                src = first.at[pl.ds(at, size)] if c == 0 else gi.at[l, xo, ko, r]
                sums = self.rv.at[slot, xo, pl.ds(at, size)]
                sums_there = self.rv.at[slot, xo, pl.ds(at, size)]
                pair = remote(src, sums_there, e_s.at[sem], e_r.at[sem], partner)
                cross = remote(sums, self.xr.at[slot, pl.ds(at, size)], x_s.at[sem], x_r.at[sem], across)
                self.parts.append((at, size, pair, cross))
            if c == 0:
                self.load_first = pltpu.make_async_copy(gi.at[l, xo, ko, r], first, lf)
            self.pair = remote(gi.at[l, x, ko, r], self.rv.at[slot, x], d_s.at[c], d_r.at[c], partner)
            self.load_b = pltpu.make_async_copy(gi.at[l, xo, k, r], self.ob, lb.at[c % 2])
            block = (l, r)
            self.loads = [
                pltpu.make_async_copy(gi.at[l, x, k, r], self.oc, lc.at[p, 0]),
                pltpu.make_async_copy(w[self.i].at[l, x, k, r], self.wc, lc.at[p, 1]),
                pltpu.make_async_copy(m[self.i].at[block], self.mc, lc.at[p, 2]),
                pltpu.make_async_copy(v[self.i].at[block], self.vc, lc.at[p, 3]),
            ]
            new, place = self.xr.at[slot], wi.at[l, x, k, r]
            self.stores = [
                pltpu.make_async_copy(self.mc, mo[self.i].at[block], st.at[p, 0]),
                pltpu.make_async_copy(self.vc, vo[self.i].at[block], st.at[p, 1]),
                pltpu.make_async_copy(new, place, st.at[p, 2]),
            ]
            self.own = remote(new, place, o_s.at[c], o_r.at[c], partner)
            self.gather = self.forward = None
            if self.i < GATHERED:
                far = wi.at[l, xo, k, r]
                self.gather = remote(new, late if c == LATE else place, ax_s.at[c], ax_r.at[c], across)
                if c != LATE:
                    self.forward = remote(far, far, f_s.at[c], f_r.at[c], partner)
            else:
                (q,) = (q for q, of in enumerate(PIECES) if j in of)
                self.stores.append(pltpu.make_async_copy(new, pieces[q].at[pl.ds((j - PIECES[q][0]) * rows, rows)], st.at[p, 3]))

    chunks = [Chunk(c) for c in range(CHUNKS)]
    chunks[0].load_first.start()
    for ch in chunks[:2]:
        ch.load_b.start()
        for one in ch.loads:
            one.start()

    barrier = pltpu.get_barrier_semaphore()
    for d in (partner, across):
        pl.semaphore_signal(barrier, inc=1, device_id=d, device_id_type=pl.DeviceIdType.MESH)
    pl.semaphore_wait(barrier, 2)

    chunks[0].load_first.wait()

    def send(ch):
        for _, _, pair, _ in ch.parts:
            pair.start()

    for ch in chunks[:AHEAD]:
        send(ch)
    for ch in chunks:
        ch.load_b.wait()
        for at, size, pair, cross in ch.parts:
            pair.wait_recv()
            add_into(ch.rv, (ch.slot, xo), ch.ob, at, size, ch.cols)
            cross.start()
        if ch.c + AHEAD < CHUNKS:
            send(chunks[ch.c + AHEAD])
        ch.pair.start()
        if ch.c + 2 < CHUNKS:
            chunks[ch.c + 2].load_b.start()
    for ch in chunks:
        for one in ch.loads:
            one.wait()
        ch.pair.wait_recv()
        for _, _, _, cross in ch.parts:
            cross.wait_recv()
        step_into(ch.xr, (ch.slot,), ch.oc, ch.rv, (ch.slot, x), ch.wc, ch.mc, ch.vc, ch.rows, ch.cols)
        if ch.gather:
            ch.gather.start()
        ch.own.start()
        for one in ch.stores:
            one.start()
        if ch.c >= 1:
            for one in chunks[ch.c - 1].stores:
                one.wait()
        if ch.c + 2 < CHUNKS:
            for one in chunks[ch.c + 2].loads:
                one.start()
    for one in chunks[-1].stores:
        one.wait()
    for ch in chunks:
        for _, _, pair, cross in ch.parts:
            pair.wait_send()
            cross.wait_send()
        ch.pair.wait_send()
        ch.own.wait()
    for ch in chunks:
        if ch.forward:
            ch.gather.wait_recv()
            ch.forward.start()
    for ch in chunks:
        if ch.forward:
            ch.gather.wait_send()
            ch.forward.wait()
    chunks[LATE].gather.wait()


def communicate(g, w, m, v):
    dims = [one.shape[3:] for one in g]
    (ra, ca), (rb, cb) = dims[0], dims[2]
    ra, rb = ra // SUBS, rb // SUBS
    sd = jax.ShapeDtypeStruct
    bf, f32 = jnp.bfloat16, jnp.float32
    dma = pltpu.SemaphoreType.DMA
    out = (
        *(sd(one.shape, bf) for one in w),
        *(sd(one.shape, f32) for one in m),
        *(sd(one.shape, f32) for one in v),
        *(sd((len(of) * rb, cb), bf) for of in PIECES),
        sd((ra, ca), bf),
    )
    scratch = [
        pltpu.VMEM((2 * PER, 2, ra, ca), bf), pltpu.VMEM((PER, 2, rb, cb), bf),
        pltpu.VMEM((2 * PER, ra, ca), bf), pltpu.VMEM((PER, rb, cb), bf),
        pltpu.VMEM((ra, ca), bf), pltpu.VMEM((2, ra, ca), bf), pltpu.VMEM((2, rb, cb), bf),
        pltpu.VMEM((SLOTS, ra, ca), bf), pltpu.VMEM((SLOTS, rb, cb), bf),
        pltpu.VMEM((SLOTS, ra, ca), bf), pltpu.VMEM((SLOTS, rb, cb), bf),
        pltpu.VMEM((SLOTS, ra, ca), f32), pltpu.VMEM((SLOTS, rb, cb), f32),
        pltpu.VMEM((SLOTS, ra, ca), f32), pltpu.VMEM((SLOTS, rb, cb), f32),
        *(dma((CHUNKS + PARTS - 1,)) for _ in range(4)),
        *(dma((CHUNKS,)) for _ in range(2)),
        *(dma((GATHERED * PER,)) for _ in range(2)),
        *(dma((CHUNKS,)) for _ in range(2)),
        *(dma((LATE,)) for _ in range(2)),
        dma, dma((2,)), dma((SLOTS, 4)), dma((SLOTS, 4)),
    ]
    return pl.pallas_call(
        functools.partial(main_kernel, dims),
        out_shape=out,
        in_specs=[ANY] * 12,
        out_specs=[ANY] * len(out),
        scratch_shapes=scratch,
        compiler_params=pltpu.CompilerParams(collective_id=0, has_side_effects=True, vmem_limit_bytes=VMEM_LIMIT),
        name="communicate",
    )(*g, *w, *m, *v)


def copy_kernel(n, _, *refs):
    for src, dst in zip(refs[:n], refs[n:], strict=True):
        dst[...] = src[...]


def copy_out(x, wf, mo, vo):
    specs = []
    for one in wf[:2]:
        rows, cols = one.shape[3:]
        specs.append(pl.BlockSpec((1, 1, 1, rows, cols), lambda i, _: (i // 4, i // 2 % 2, i % 2, 0, 0)))
    rows, cols = wf[2].shape[3:]
    specs.append(pl.BlockSpec((1, 1, 1, rows // 2, cols), lambda i, s: (i // 4, s[0], i // 2 % 2, i % 2, 0)))
    for one in (*mo, *vo):
        _, rows, cols = one.shape
        specs.append(pl.BlockSpec((1, rows // SUBS, cols), lambda i, _: (i // SUBS, i % SUBS, 0)))
    arrays = (*wf, *mo, *vo)
    size = sum(2 * one.size * one.dtype.itemsize for one in arrays)
    return pl.pallas_call(
        functools.partial(copy_kernel, len(arrays)),
        out_shape=[jax.ShapeDtypeStruct(one.shape, one.dtype) for one in arrays],
        grid_spec=pltpu.PrefetchScalarGridSpec(num_scalar_prefetch=1, grid=(PER,), in_specs=specs, out_specs=specs),
        cost_estimate=pl.CostEstimate(flops=0, bytes_accessed=size, transcendentals=0),
        compiler_params=pltpu.CompilerParams(vmem_limit_bytes=VMEM_ALL),
        name="copy_out",
    )(x.reshape(1), *arrays)


def place_kernel(l, first, near, far, whole, out, buf, ld, st):
    me = lax.axis_index("dp")
    x, k = me // 2, me % 2
    r = pl.ds(first, near.shape[0])
    loads = [pltpu.make_async_copy(near, buf.at[0], ld.at[0]), pltpu.make_async_copy(far, buf.at[1], ld.at[1])]
    stores = [
        pltpu.make_async_copy(buf.at[0], out.at[l, 1 - x, k, r], st.at[0]),
        pltpu.make_async_copy(buf.at[1], out.at[l, 1 - x, 1 - k, r], st.at[1]),
    ]
    for one in loads:
        one.start()
    for a, b in zip(loads, stores, strict=True):
        a.wait()
        b.start()
    for one in stores:
        one.wait()


def place(l, first, near, far, whole):
    return pl.pallas_call(
        functools.partial(place_kernel, l, first),
        out_shape=jax.ShapeDtypeStruct(whole.shape, whole.dtype),
        in_specs=[ANY] * 3,
        out_specs=ANY,
        scratch_shapes=[pltpu.VMEM((2, *near.shape), whole.dtype), pltpu.SemaphoreType.DMA((2,)), pltpu.SemaphoreType.DMA((2,))],
        input_output_aliases={2: 0},
        cost_estimate=pl.CostEstimate(flops=0, bytes_accessed=8 * near.size, transcendentals=0),
        compiler_params=pltpu.CompilerParams(vmem_limit_bytes=VMEM_ALL),
        name="place",
    )(near, far, whole)


def solution(mesh):
    swap_x, swap_core = [(i, (i + 2) % 4) for i in range(4)], [(i, i ^ 1) for i in range(4)]

    def step(*arrays):
        terms, weights, m, v = (arrays[i : i + 3] for i in (0, 3, 6, 9))

        def cut(a):
            return a.reshape(LAYERS, 2, 2, a.shape[-2] // 4, a.shape[-1])

        done = communicate([cut(t) for t in terms], [cut(w) for w in weights], m, v)
        wf, mo, vo, pieces, late = done[:3], done[3:6], done[6:9], done[9:-1], done[-1]
        cross = []
        for p in pieces:
            cross.append(lax.ppermute(p, "dp", swap_x))
        late_far = lax.ppermute(late, "dp", swap_core)
        x = (lax.axis_index("dp") // 2).astype(jnp.int32)
        gate, up, down, *moments = copy_out(x, wf, mo, vo)
        up = place(LAYERS - 1, (SUBS - 1) * late.shape[0], late, late_far, up)
        up, down = lax.optimization_barrier((up, down))
        for i, p in enumerate(cross):
            p, down = lax.optimization_barrier((p, down))
            far = lax.ppermute(p, "dp", swap_core)
            l, sub = PIECES[i][0] // SUBS, PIECES[i][0] % SUBS
            down = place(l, sub * p.shape[0] // len(PIECES[i]), p, far, down)
        whole = [a.reshape(w.shape) for a, w in zip((gate, up, down), weights, strict=True)]
        return (*whole, *moments)

    all_of, cut = P(None, None, None), P(None, "dp", None)
    return jax.shard_map(
        step,
        mesh=mesh,
        in_specs=(P(("rep", "dp"), None, None, None),) * 3 + (all_of,) * 3 + (cut,) * 6,
        out_specs=(P("rep", None, None),) * 3 + (P("rep", "dp", None),) * 6,
        check_vma=False,
    )
```

profile of v0, /device:TPU:0, one launch (start us, length us, event | category | flops | bytes accessed | tf_op | source)
XLA Modules:
  0.0 427.2 jit_solution(3018367060761696847)
XLA Ops:
  0.6 319.4 %communicate.1 = (bf16[2,2,2,256,2816]{4,3,2,1,0:T(8,128)(2,1)}, bf16[2,2,2,256,2816]{4,3,2,1,0:T(8,128)(2,1)}, bf16[2,2,2,704,1024]{4,3,2,1,0:T(8,128)(2,1)}, f...) custom-call(bf16[2,2,2,256,2816]{4,3,2,1,0:T(8,128)(2,1)} %bitcast.1, ...), custom_call_target="tpu_custom_call" | custom-call | tf_op jit(solution)/shard_map/communicate/pallas_call | solution.py:221
  320.0 0.0 collective-permute-start.5
  320.1 0.1 collective-permute-start
  320.2 41.0 %copy_out.1 = (bf16[2,2,2,256,2816]{4,3,2,1,0:T(8,128)(2,1)}, bf16[2,2,2,256,2816]{4,3,2,1,0:T(8,128)(2,1)}, bf16[2,2,2,704,1024]{4,3,2,1,0:T(8,128)(2,1)}, f32[...) custom-call(s32[1]{0:T(128)} %bitcast._, ...), custom_call_target="tpu_custom_call" | custom-call | bytes 138412032 | tf_op jit(solution)/shard_map/copy_out/pallas_call | solution.py:249
  361.2 0.0 collective-permute-done.far
  361.2 1.9 place.6
  363.1 0.0 collective-permute-done.5.near
  363.1 0.4 collective-permute-start.6
  363.5 2.0 collective-permute-start.4
  365.5 0.2 collective-permute-done.6.far
  365.7 2.2 place.7.whole
  367.9 14.2 %collective-permute-done.4.near = bf16[352,1024]{1,0:T(8,128)(2,1)} collective-permute-done((bf16[352,1024]{1,0:T(8,128)(2,1)}, bf16[352,1024]{1,0:T(8,128)(2,1)}, u32[]{:S(2)}, u32[]{:S(2)}) %collective-permute-start.4) | collective-permute-done | bytes 720928 | tf_op jit(solution)/shard_map/ppermute | solution.py:304
  382.2 0.0 collective-permute-start.7
  382.2 1.7 collective-permute-start.3
  383.9 0.8 collective-permute-done.7.far
  384.7 2.2 place.8.whole
  387.0 14.1 %collective-permute-done.3.near = bf16[352,1024]{1,0:T(8,128)(2,1)} collective-permute-done((bf16[352,1024]{1,0:T(8,128)(2,1)}, bf16[352,1024]{1,0:T(8,128)(2,1)}, u32[]{:S(2)}, u32[]{:S(2)}) %collective-permute-start.3) | collective-permute-done | bytes 720928 | tf_op jit(solution)/shard_map/ppermute | solution.py:304
  401.0 0.0 collective-permute-start.8
  401.1 1.7 collective-permute-start.2
  402.8 0.8 collective-permute-done.8.far
  403.6 2.2 place.9.whole
  405.8 6.4 %collective-permute-done.2.near = bf16[176,1024]{1,0:T(8,128)(2,1)} collective-permute-done((bf16[176,1024]{1,0:T(8,128)(2,1)}, bf16[176,1024]{1,0:T(8,128)(2,1)}, u32[]{:S(2)}, u32[]{:S(2)}) %collective-permute-start.2) | collective-permute-done | bytes 360480 | tf_op jit(solution)/shard_map/ppermute | solution.py:304
  412.2 0.0 collective-permute-start.9
  412.2 1.7 collective-permute-start.1
  413.9 0.3 collective-permute-done.9.far
  414.2 1.9 place.10.whole
  416.1 7.2 %collective-permute-done.1.near = bf16[176,1024]{1,0:T(8,128)(2,1)} collective-permute-done((bf16[176,1024]{1,0:T(8,128)(2,1)}, bf16[176,1024]{1,0:T(8,128)(2,1)}, u32[]{:S(2)}, u32[]{:S(2)}) %collective-permute-start.1) | collective-permute-done | bytes 360480 | tf_op jit(solution)/shard_map/ppermute | solution.py:304
  423.3 0.0 collective-permute-start.10
  423.3 2.0 collective-permute-done.10.far
  425.4 1.9 place.11
Async XLA Ops:
  320.0 43.1 %collective-permute-start.5 = (bf16[352,1024]{1,0:T(8,128)(2,1)}, bf16[352,1024]{1,0:T(8,128)(2,1)}, u32[]{:S(2)}, u32[]{:S(2)}) collective-permute-start(bf16[352,1024]{1,0:T(8,128)(2,1)} %get-tuple-element.63), channel_id=1, source_target_pairs={{0,2},{1,3},{2,0},{3,1},{4,6},{5,7},{6,4},{7,5}} | collective-permute-start | bytes 2162696 | tf_op jit(solution)/shard_map/ppermute | solution.py:304
  320.1 41.1 %collective-permute-start = (bf16[64,2816]{1,0:T(8,128)(2,1)}, bf16[64,2816]{1,0:T(8,128)(2,1)}, u32[]{:S(2)}, u32[]{:S(2)}) collective-permute-start(bf16[64,2816]{1,0:T(8,128)(2,1)} %get-tuple-element.55.near), channel_id=1, source_target_pairs={{0,1},{1,0},{2,3},{3,2},{4,5},{5,4},{6,7},{7,6}} | collective-permute-start | bytes 1081352 | tf_op jit(solution)/shard_map/ppermute | solution.py:305
  363.1 2.6 collective-permute-start.6
  363.5 18.6 %collective-permute-start.4 = (bf16[352,1024]{1,0:T(8,128)(2,1)}, bf16[352,1024]{1,0:T(8,128)(2,1)}, u32[]{:S(2)}, u32[]{:S(2)}) collective-permute-start(bf16[352,1024]{1,0:T(8,128)(2,1)} %get-tuple-element.62), channel_id=1, source_target_pairs={{0,2},{1,3},{2,0},{3,1},{4,6},{5,7},{6,4},{7,5}} | collective-permute-start | bytes 2162696 | tf_op jit(solution)/shard_map/ppermute | solution.py:304
  382.2 2.5 collective-permute-start.7
  382.2 18.9 %collective-permute-start.3 = (bf16[352,1024]{1,0:T(8,128)(2,1)}, bf16[352,1024]{1,0:T(8,128)(2,1)}, u32[]{:S(2)}, u32[]{:S(2)}) collective-permute-start(bf16[352,1024]{1,0:T(8,128)(2,1)} %get-tuple-element.61), channel_id=1, source_target_pairs={{0,2},{1,3},{2,0},{3,1},{4,6},{5,7},{6,4},{7,5}} | collective-permute-start | bytes 2162696 | tf_op jit(solution)/shard_map/ppermute | solution.py:304
  401.0 2.5 collective-permute-start.8
  401.1 11.1 %collective-permute-start.2 = (bf16[176,1024]{1,0:T(8,128)(2,1)}, bf16[176,1024]{1,0:T(8,128)(2,1)}, u32[]{:S(2)}, u32[]{:S(2)}) collective-permute-start(bf16[176,1024]{1,0:T(8,128)(2,1)} %get-tuple-element.60), channel_id=1, source_target_pairs={{0,2},{1,3},{2,0},{3,1},{4,6},{5,7},{6,4},{7,5}} | collective-permute-start | bytes 1081352 | tf_op jit(solution)/shard_map/ppermute | solution.py:304
  412.2 2.0 collective-permute-start.9
  412.2 11.1 %collective-permute-start.1 = (bf16[176,1024]{1,0:T(8,128)(2,1)}, bf16[176,1024]{1,0:T(8,128)(2,1)}, u32[]{:S(2)}, u32[]{:S(2)}) collective-permute-start(bf16[176,1024]{1,0:T(8,128)(2,1)} %get-tuple-element.59), channel_id=1, source_target_pairs={{0,2},{1,3},{2,0},{3,1},{4,6},{5,7},{6,4},{7,5}} | collective-permute-start | bytes 1081352 | tf_op jit(solution)/shard_map/ppermute | solution.py:304
  423.3 2.0 collective-permute-start.10
where the time goes:
time: 428 us; the launch traced here: 427 us
  Pallas kernels  373 us (87%)
  waiting for transfers between devices  46 us (11%)
  starting transfers between devices  7.8 us (2%)
    pallas_call x1, Pallas kernels, communicate(): pl.pallas_call(functools.partial(main_kernel, dims), out_shape=out, in_sp...  319 us
    ppermute x5, waiting for transfers between devices, step(): cross.append(lax.ppermute(p, 'dp', swap_x))  41.9 us
    pallas_call x1, Pallas kernels, copy_out(): pl.pallas_call(functools.partial(copy_kernel, len(arrays)), out_shape=[ja...  41 us
    pallas_call x6, Pallas kernels, place(): pl.pallas_call(functools.partial(place_kernel, l, first), out_shape=jax.S...  12.3 us
  transfers between devices with their start and end apart: 11, of which 9 were waited for; matrix products, arithmetic and copies ran while one was open for 0% of the time, Pallas kernels for 12%

commit v1 on v0

--- a/solution.py
+++ b/solution.py
@@ -17,7 +17,7 @@
 SLOTS = 3
 AHEAD = 4
 PARTS = 4
-PIECES = ((0, 1), (2, 3), (4, 5), (6,), (7,))
+PIECES = ((0, 0, 416), (0, 416, 288), (1, 0, 384), (1, 384, 208), (1, 592, 112))
 LATE = GATHERED * PER - 1
 ANY = pl.BlockSpec(memory_space=pl.ANY)
 VMEM_LIMIT = 60 * 2**20
@@ -59,8 +59,8 @@
     g, w, m, v = (refs[i : i + 3] for i in (0, 3, 6, 9))
     wf, mo, vo = (refs[12 + i : 15 + i] for i in (0, 3, 6))
     pieces, late = refs[21 : 21 + len(PIECES)], refs[21 + len(PIECES)]
-    (rv_a, rv_b, xr_a, xr_b, first, ob_a, ob_b, oc_a, oc_b, wc_a, wc_b, mc_a, mc_b, vc_a, vc_b,
-     e_s, e_r, x_s, x_r, d_s, d_r, ax_s, ax_r, o_s, o_r, f_s, f_r, lf, lb, lc, st) = refs[22 + len(PIECES) :]
+    (rv_a, rv_b, xr_a, xr_b, ob_a, ob_b, oc_a, oc_b, wc_a, wc_b, mc_a, mc_b, vc_a, vc_b,
+     e_s, e_r, x_s, x_r, d_s, d_r, ax_s, ax_r, o_s, o_r, f_s, f_r, lb, lc, st) = refs[22 + len(PIECES) :]
     me = lax.axis_index("dp")
     x, k = me // 2, me % 2
     xo, ko = 1 - x, 1 - k
@@ -87,14 +87,12 @@
             self.parts = []
             for q in range(n):
                 at, size, sem = q * rows // n, rows // n, q if c == 0 else c + PARTS - 1
-                src = first.at[pl.ds(at, size)] if c == 0 else gi.at[l, xo, ko, r]
+                src = gi.at[l, xo, ko, pl.ds(sub * rows + at, size)]
                 sums = self.rv.at[slot, xo, pl.ds(at, size)]
                 sums_there = self.rv.at[slot, xo, pl.ds(at, size)]
                 pair = remote(src, sums_there, e_s.at[sem], e_r.at[sem], partner)
                 cross = remote(sums, self.xr.at[slot, pl.ds(at, size)], x_s.at[sem], x_r.at[sem], across)
                 self.parts.append((at, size, pair, cross))
-            if c == 0:
-                self.load_first = pltpu.make_async_copy(gi.at[l, xo, ko, r], first, lf)
             self.pair = remote(gi.at[l, x, ko, r], self.rv.at[slot, x], d_s.at[c], d_r.at[c], partner)
             self.load_b = pltpu.make_async_copy(gi.at[l, xo, k, r], self.ob, lb.at[c % 2])
             block = (l, r)
@@ -118,29 +116,27 @@
                 if c != LATE:
                     self.forward = remote(far, far, f_s.at[c], f_r.at[c], partner)
             else:
-                (q,) = (q for q, of in enumerate(PIECES) if j in of)
-                self.stores.append(pltpu.make_async_copy(new, pieces[q].at[pl.ds((j - PIECES[q][0]) * rows, rows)], st.at[p, 3]))
+                for q, (layer, top, size) in enumerate(PIECES):
+                    low, high = max(top, sub * rows), min(top + size, (sub + 1) * rows)
+                    if layer == l and low < high:
+                        part = new.at[pl.ds(low - sub * rows, high - low)]
+                        self.stores.append(pltpu.make_async_copy(part, pieces[q].at[pl.ds(low - top, high - low)], st.at[p, len(self.stores)]))
 
     chunks = [Chunk(c) for c in range(CHUNKS)]
-    chunks[0].load_first.start()
-    for ch in chunks[:2]:
-        ch.load_b.start()
-        for one in ch.loads:
-            one.start()
+    chunks[0].load_b.start()
 
     barrier = pltpu.get_barrier_semaphore()
     for d in (partner, across):
         pl.semaphore_signal(barrier, inc=1, device_id=d, device_id_type=pl.DeviceIdType.MESH)
     pl.semaphore_wait(barrier, 2)
 
-    chunks[0].load_first.wait()
-
     def send(ch):
         for _, _, pair, _ in ch.parts:
             pair.start()
 
     for ch in chunks[:AHEAD]:
         send(ch)
+    chunks[1].load_b.start()
     for ch in chunks:
         ch.load_b.wait()
         for at, size, pair, cross in ch.parts:
@@ -152,6 +148,9 @@
         ch.pair.start()
         if ch.c + 2 < CHUNKS:
             chunks[ch.c + 2].load_b.start()
+    for ch in chunks[:2]:
+        for one in ch.loads:
+            one.start()
     for ch in chunks:
         for one in ch.loads:
             one.wait()
@@ -200,13 +199,13 @@
         *(sd(one.shape, bf) for one in w),
         *(sd(one.shape, f32) for one in m),
         *(sd(one.shape, f32) for one in v),
-        *(sd((len(of) * rb, cb), bf) for of in PIECES),
+        *(sd((size, cb), bf) for _, _, size in PIECES),
         sd((ra, ca), bf),
     )
     scratch = [
         pltpu.VMEM((2 * PER, 2, ra, ca), bf), pltpu.VMEM((PER, 2, rb, cb), bf),
         pltpu.VMEM((2 * PER, ra, ca), bf), pltpu.VMEM((PER, rb, cb), bf),
-        pltpu.VMEM((ra, ca), bf), pltpu.VMEM((2, ra, ca), bf), pltpu.VMEM((2, rb, cb), bf),
+        pltpu.VMEM((2, ra, ca), bf), pltpu.VMEM((2, rb, cb), bf),
         pltpu.VMEM((SLOTS, ra, ca), bf), pltpu.VMEM((SLOTS, rb, cb), bf),
         pltpu.VMEM((SLOTS, ra, ca), bf), pltpu.VMEM((SLOTS, rb, cb), bf),
         pltpu.VMEM((SLOTS, ra, ca), f32), pltpu.VMEM((SLOTS, rb, cb), f32),
@@ -216,7 +215,7 @@
         *(dma((GATHERED * PER,)) for _ in range(2)),
         *(dma((CHUNKS,)) for _ in range(2)),
         *(dma((LATE,)) for _ in range(2)),
-        dma, dma((2,)), dma((SLOTS, 4)), dma((SLOTS, 4)),
+        dma((2,)), dma((SLOTS, 4)), dma((SLOTS, 5)),
     ]
     return pl.pallas_call(
         functools.partial(main_kernel, dims),
@@ -310,8 +309,7 @@
         for i, p in enumerate(cross):
             p, down = lax.optimization_barrier((p, down))
             far = lax.ppermute(p, "dp", swap_core)
-            l, sub = PIECES[i][0] // SUBS, PIECES[i][0] % SUBS
-            down = place(l, sub * p.shape[0] // len(PIECES[i]), p, far, down)
+            down = place(*PIECES[i][:2], p, far, down)
         whole = [a.reshape(w.shape) for a, w in zip((gate, up, down), weights, strict=True)]
         return (*whole, *moments)
 

time: 428 us -> 420 us (0.981)
    ppermute x5, waiting for transfers between devices: 41.9 us -> 35.1 us  [step(): cross.append(lax.ppermute(p, 'dp', swap_x))]
where the time goes in v1:
time: 420 us
  Pallas kernels  371 us (88%)
  waiting for transfers between devices  43.3 us (10%)
  starting transfers between devices  5.16 us (1%)
    pallas_call x1, Pallas kernels, communicate(): pl.pallas_call(functools.partial(main_kernel, dims), out_shape=out, in_sp...  317 us
    pallas_call x1, Pallas kernels, copy_out(): pl.pallas_call(functools.partial(copy_kernel, len(arrays)), out_shape=[ja...  41 us
    ppermute x5, waiting for transfers between devices, step(): cross.append(lax.ppermute(p, 'dp', swap_x))  35.1 us
    pallas_call x6, Pallas kernels, place(): pl.pallas_call(functools.partial(place_kernel, l, first), out_shape=jax.S...  12.4 us
  transfers between devices with their start and end apart: 11, of which 9 were waited for; matrix products, arithmetic and copies ran while one was open for 0% of the time, Pallas kernels for 12%

profile of v1, /device:TPU:0, one launch (start us, length us, event | category | flops | bytes accessed | tf_op | source)
XLA Modules:
  0.0 420.0 jit_solution(17171211882574847193)
XLA Ops:
  0.6 317.4 %communicate.1 = (bf16[2,2,2,256,2816]{4,3,2,1,0:T(8,128)(2,1)}, bf16[2,2,2,256,2816]{4,3,2,1,0:T(8,128)(2,1)}, bf16[2,2,2,704,1024]{4,3,2,1,0:T(8,128)(2,1)}, f...) custom-call(bf16[2,2,2,256,2816]{4,3,2,1,0:T(8,128)(2,1)} %bitcast.1, ...), custom_call_target="tpu_custom_call" | custom-call | tf_op jit(solution)/shard_map/communicate/pallas_call | solution.py:220
  318.1 1.5 collective-permute-start.5
  319.6 0.0 collective-permute-start
  319.6 41.0 %copy_out.1 = (bf16[2,2,2,256,2816]{4,3,2,1,0:T(8,128)(2,1)}, bf16[2,2,2,256,2816]{4,3,2,1,0:T(8,128)(2,1)}, bf16[2,2,2,704,1024]{4,3,2,1,0:T(8,128)(2,1)}, f32[...) custom-call(s32[1]{0:T(128)} %bitcast._, ...), custom_call_target="tpu_custom_call" | custom-call | bytes 138412032 | tf_op jit(solution)/shard_map/copy_out/pallas_call | solution.py:248
  360.6 0.0 collective-permute-done.far
  360.6 1.9 place.6
  362.5 0.0 collective-permute-done.5.near
  362.5 0.5 collective-permute-start.6
  363.1 0.5 collective-permute-start.4
  363.6 1.5 collective-permute-start.3
  365.1 0.3 collective-permute-done.6.far
  365.4 2.4 place.7.whole
  367.8 11.8 %collective-permute-done.4.near = bf16[288,1024]{1,0:T(8,128)(2,1)} collective-permute-done((bf16[288,1024]{1,0:T(8,128)(2,1)}, bf16[288,1024]{1,0:T(8,128)(2,1)}, u32[]{:S(2)}, u32[]{:S(2)}) %collective-permute-start.4) | collective-permute-done | bytes 589856 | tf_op jit(solution)/shard_map/ppermute | solution.py:303
  379.6 0.0 collective-permute-start.7
  379.6 2.3 collective-permute-done.7.far
  381.9 2.1 place.8.whole
  384.0 11.5 %collective-permute-done.3.near = bf16[384,1024]{1,0:T(8,128)(2,1)} collective-permute-done((bf16[384,1024]{1,0:T(8,128)(2,1)}, bf16[384,1024]{1,0:T(8,128)(2,1)}, u32[]{:S(2)}, u32[]{:S(2)}) %collective-permute-start.3) | collective-permute-done | bytes 786464 | tf_op jit(solution)/shard_map/ppermute | solution.py:303
  395.5 0.0 collective-permute-start.8
  395.5 0.5 collective-permute-start.2
  396.0 2.1 collective-permute-done.8.far
  398.1 2.3 place.9.whole
  400.4 7.6 %collective-permute-done.2.near = bf16[208,1024]{1,0:T(8,128)(2,1)} collective-permute-done((bf16[208,1024]{1,0:T(8,128)(2,1)}, bf16[208,1024]{1,0:T(8,128)(2,1)}, u32[]{:S(2)}, u32[]{:S(2)}) %collective-permute-start.2) | collective-permute-done | bytes 426016 | tf_op jit(solution)/shard_map/ppermute | solution.py:303
  408.0 0.0 collective-permute-start.9
  408.0 0.5 collective-permute-start.1
  408.6 1.6 collective-permute-done.9.far
  410.2 1.9 place.10.whole
  412.1 4.3 %collective-permute-done.1.near = bf16[112,1024]{1,0:T(8,128)(2,1)} collective-permute-done((bf16[112,1024]{1,0:T(8,128)(2,1)}, bf16[112,1024]{1,0:T(8,128)(2,1)}, u32[]{:S(2)}, u32[]{:S(2)}) %collective-permute-start.1) | collective-permute-done | bytes 229408 | tf_op jit(solution)/shard_map/ppermute | solution.py:303
  416.4 0.0 collective-permute-start.10
  416.4 1.8 collective-permute-done.10.far
  418.2 1.8 place.11
Async XLA Ops:
  318.1 44.4 %collective-permute-start.5 = (bf16[416,1024]{1,0:T(8,128)(2,1)}, bf16[416,1024]{1,0:T(8,128)(2,1)}, u32[]{:S(2)}, u32[]{:S(2)}) collective-permute-start(bf16[416,1024]{1,0:T(8,128)(2,1)} %get-tuple-element.63), channel_id=1, source_target_pairs={{0,2},{1,3},{2,0},{3,1},{4,6},{5,7},{6,4},{7,5}} | collective-permute-start | bytes 2555912 | tf_op jit(solution)/shard_map/ppermute | solution.py:303
  319.6 41.0 %collective-permute-start = (bf16[64,2816]{1,0:T(8,128)(2,1)}, bf16[64,2816]{1,0:T(8,128)(2,1)}, u32[]{:S(2)}, u32[]{:S(2)}) collective-permute-start(bf16[64,2816]{1,0:T(8,128)(2,1)} %get-tuple-element.55.near), channel_id=1, source_target_pairs={{0,1},{1,0},{2,3},{3,2},{4,5},{5,4},{6,7},{7,6}} | collective-permute-start | bytes 1081352 | tf_op jit(solution)/shard_map/ppermute | solution.py:304
  362.5 2.9 collective-permute-start.6
  363.1 16.5 %collective-permute-start.4 = (bf16[288,1024]{1,0:T(8,128)(2,1)}, bf16[288,1024]{1,0:T(8,128)(2,1)}, u32[]{:S(2)}, u32[]{:S(2)}) collective-permute-start(bf16[288,1024]{1,0:T(8,128)(2,1)} %get-tuple-element.62), channel_id=1, source_target_pairs={{0,2},{1,3},{2,0},{3,1},{4,6},{5,7},{6,4},{7,5}} | collective-permute-start | bytes 1769480 | tf_op jit(solution)/shard_map/ppermute | solution.py:303
  363.6 31.9 %collective-permute-start.3 = (bf16[384,1024]{1,0:T(8,128)(2,1)}, bf16[384,1024]{1,0:T(8,128)(2,1)}, u32[]{:S(2)}, u32[]{:S(2)}) collective-permute-start(bf16[384,1024]{1,0:T(8,128)(2,1)} %get-tuple-element.61), channel_id=1, source_target_pairs={{0,2},{1,3},{2,0},{3,1},{4,6},{5,7},{6,4},{7,5}} | collective-permute-start | bytes 2359304 | tf_op jit(solution)/shard_map/ppermute | solution.py:303
  379.6 2.3 collective-permute-start.7
  395.5 2.6 collective-permute-start.8
  395.5 12.5 %collective-permute-start.2 = (bf16[208,1024]{1,0:T(8,128)(2,1)}, bf16[208,1024]{1,0:T(8,128)(2,1)}, u32[]{:S(2)}, u32[]{:S(2)}) collective-permute-start(bf16[208,1024]{1,0:T(8,128)(2,1)} %get-tuple-element.60), channel_id=1, source_target_pairs={{0,2},{1,3},{2,0},{3,1},{4,6},{5,7},{6,4},{7,5}} | collective-permute-start | bytes 1277960 | tf_op jit(solution)/shard_map/ppermute | solution.py:303
  408.0 2.1 collective-permute-start.9
  408.0 8.3 %collective-permute-start.1 = (bf16[112,1024]{1,0:T(8,128)(2,1)}, bf16[112,1024]{1,0:T(8,128)(2,1)}, u32[]{:S(2)}, u32[]{:S(2)}) collective-permute-start(bf16[112,1024]{1,0:T(8,128)(2,1)} %get-tuple-element.59), channel_id=1, source_target_pairs={{0,2},{1,3},{2,0},{3,1},{4,6},{5,7},{6,4},{7,5}} | collective-permute-start | bytes 688136 | tf_op jit(solution)/shard_map/ppermute | solution.py:303
  416.4 1.8 collective-permute-start.10

commit v2 on v1

--- a/solution.py
+++ b/solution.py
@@ -17,11 +17,10 @@
 SLOTS = 3
 AHEAD = 4
 PARTS = 4
-PIECES = ((0, 0, 416), (0, 416, 288), (1, 0, 384), (1, 384, 208), (1, 592, 112))
+PIECES = ((0, 0, 704), (1, 0, 480), (1, 480, 144), (1, 624, 80))
 LATE = GATHERED * PER - 1
 ANY = pl.BlockSpec(memory_space=pl.ANY)
 VMEM_LIMIT = 60 * 2**20
-VMEM_ALL = 67043328
 WIDTH = 256
 
 
@@ -250,25 +249,21 @@
         out_shape=[jax.ShapeDtypeStruct(one.shape, one.dtype) for one in arrays],
         grid_spec=pltpu.PrefetchScalarGridSpec(num_scalar_prefetch=1, grid=(PER,), in_specs=specs, out_specs=specs),
         cost_estimate=pl.CostEstimate(flops=0, bytes_accessed=size, transcendentals=0),
-        compiler_params=pltpu.CompilerParams(vmem_limit_bytes=VMEM_ALL),
+        compiler_params=pltpu.CompilerParams(vmem_limit_bytes=40 * 2**20),
         name="copy_out",
     )(x.reshape(1), *arrays)
 
 
-def place_kernel(l, first, near, far, whole, out, buf, ld, st):
+def place_kernel(l, first, near, far, whole, out, st):
     me = lax.axis_index("dp")
     x, k = me // 2, me % 2
     r = pl.ds(first, near.shape[0])
-    loads = [pltpu.make_async_copy(near, buf.at[0], ld.at[0]), pltpu.make_async_copy(far, buf.at[1], ld.at[1])]
     stores = [
-        pltpu.make_async_copy(buf.at[0], out.at[l, 1 - x, k, r], st.at[0]),
-        pltpu.make_async_copy(buf.at[1], out.at[l, 1 - x, 1 - k, r], st.at[1]),
+        pltpu.make_async_copy(near, out.at[l, 1 - x, k, r], st.at[0]),
+        pltpu.make_async_copy(far, out.at[l, 1 - x, 1 - k, r], st.at[1]),
     ]
-    for one in loads:
+    for one in stores:
         one.start()
-    for a, b in zip(loads, stores, strict=True):
-        a.wait()
-        b.start()
     for one in stores:
         one.wait()
 
@@ -277,12 +272,12 @@
     return pl.pallas_call(
         functools.partial(place_kernel, l, first),
         out_shape=jax.ShapeDtypeStruct(whole.shape, whole.dtype),
-        in_specs=[ANY] * 3,
+        in_specs=[pl.BlockSpec(memory_space=pltpu.VMEM)] * 2 + [ANY],
         out_specs=ANY,
-        scratch_shapes=[pltpu.VMEM((2, *near.shape), whole.dtype), pltpu.SemaphoreType.DMA((2,)), pltpu.SemaphoreType.DMA((2,))],
+        scratch_shapes=[pltpu.SemaphoreType.DMA((2,))],
         input_output_aliases={2: 0},
         cost_estimate=pl.CostEstimate(flops=0, bytes_accessed=8 * near.size, transcendentals=0),
-        compiler_params=pltpu.CompilerParams(vmem_limit_bytes=VMEM_ALL),
+        compiler_params=pltpu.CompilerParams(vmem_limit_bytes=2 * 2**20),
         name="place",
     )(near, far, whole)
 

time: 420 us -> 406 us (0.967)
  Pallas kernels: 371 us -> 359 us
  waiting for transfers between devices: 43.3 us -> 36.3 us
  local copies, waits for them, and re-layouts: 0 us -> 5.3 us
    pallas_call x6 -> x5, Pallas kernels: 12.4 us -> 5.33 us  [place(): pl.pallas_call(functools.partial(place_kernel, l, first), out_shape=jax.S...]
    ppermute x5 -> x4, waiting for transfers between devices: 35.1 us -> 29.5 us  [step(): cross.append(lax.ppermute(p, 'dp', swap_x))]
    unnamed x0 -> x12, local copies, waits for them, and re-layouts: none -> 5.3 us
    pallas_call x1, Pallas kernels: 41 us -> 36.7 us  [copy_out(): pl.pallas_call(functools.partial(copy_kernel, len(arrays)), out_shape=[ja...]
  transfers between devices with their start and end apart: 11 -> 9, of which waited for: 9 -> 7; matrix products, arithmetic and copies ran while one was open for 0% -> 0% of each run, Pallas kernels for 12% -> 10%
where the time goes in v2:
time: 406 us; the launch traced here: 405 us
  Pallas kernels  359 us (88%)
  waiting for transfers between devices  36.3 us (9%)
  local copies, waits for them, and re-layouts  5.3 us (1%)
    pallas_call x1, Pallas kernels, communicate(): pl.pallas_call(functools.partial(main_kernel, dims), out_shape=out, in_sp...  317 us
    pallas_call x1, Pallas kernels, copy_out(): pl.pallas_call(functools.partial(copy_kernel, len(arrays)), out_shape=[ja...  36.7 us
    ppermute x4, waiting for transfers between devices, step(): cross.append(lax.ppermute(p, 'dp', swap_x))  29.5 us
  transfers between devices with their start and end apart: 9, of which 7 were waited for; matrix products, arithmetic and copies ran while one was open for 0% of the time, Pallas kernels for 10%

profile of v2, /device:TPU:0, one launch (start us, length us, event | category | flops | bytes accessed | tf_op | source)
XLA Modules:
  0.0 405.4 jit_solution(527465852621735551)
XLA Ops:
  0.6 317.4 %communicate.1 = (bf16[2,2,2,256,2816]{4,3,2,1,0:T(8,128)(2,1)}, bf16[2,2,2,256,2816]{4,3,2,1,0:T(8,128)(2,1)}, bf16[2,2,2,704,1024]{4,3,2,1,0:T(8,128)(2,1)}, f...) custom-call(bf16[2,2,2,256,2816]{4,3,2,1,0:T(8,128)(2,1)} %bitcast.1, ...), custom_call_target="tpu_custom_call" | custom-call | tf_op jit(solution)/shard_map/communicate/pallas_call | solution.py:219
  318.1 1.5 collective-permute-start.4
  319.6 0.0 collective-permute-start
  319.6 2.6 copy-done
  322.2 2.6 copy-done.1
  324.9 36.7 %copy_out.1 = (bf16[2,2,2,256,2816]{4,3,2,1,0:T(8,128)(2,1)}, bf16[2,2,2,256,2816]{4,3,2,1,0:T(8,128)(2,1)}, bf16[2,2,2,704,1024]{4,3,2,1,0:T(8,128)(2,1)}, f32[...) custom-call(s32[1]{0:T(128)} %bitcast._, ...), custom_call_target="tpu_custom_call" | custom-call | bytes 138412032 | tf_op jit(solution)/shard_map/copy_out/pallas_call | solution.py:247
  361.5 0.0 collective-permute-done.far
  361.5 0.0 copy-done.2
  361.6 0.0 copy-start.3
  361.6 0.9 place.5
  362.5 0.0 collective-permute-done.4.near
  362.5 0.5 collective-permute-start.5
  363.0 0.0 copy-done.3
  363.0 0.5 collective-permute-start.3
  363.6 2.3 collective-permute-done.5.far
  365.9 1.6 place.6.whole
  367.4 19.7 %collective-permute-done.3.near = bf16[480,1024]{1,0:T(8,128)(2,1)S(1)} collective-permute-done((bf16[480,1024]{1,0:T(8,128)(2,1)S(1)}, bf16[480,1024]{1,0:T(8,128)(2,1)S(1)}, u32[]{:S(2)}, u32[]{:S(2)}) %collective-permute-start.3) | collective-permute-done | bytes 983072 | tf_op jit(solution)/shard_map/ppermute | solution.py:298
  387.2 0.0 collective-permute-start.6
  387.2 0.0 copy-done.4
  387.2 0.6 collective-permute-start.2
  387.8 2.0 collective-permute-done.6.far
  389.8 1.3 place.7.whole
  391.0 5.6 %collective-permute-done.2.near = bf16[144,1024]{1,0:T(8,128)(2,1)S(1)} collective-permute-done((bf16[144,1024]{1,0:T(8,128)(2,1)S(1)}, bf16[144,1024]{1,0:T(8,128)(2,1)S(1)}, u32[]{:S(2)}, u32[]{:S(2)}) %collective-permute-start.2) | collective-permute-done | bytes 294944 | tf_op jit(solution)/shard_map/ppermute | solution.py:298
  396.6 0.0 collective-permute-start.7
  396.6 0.0 copy-done.5
  396.6 0.5 collective-permute-start.1
  397.2 1.0 collective-permute-done.7.far
  398.2 0.8 place.8.whole
  399.0 4.2 %collective-permute-done.1.near = bf16[80,1024]{1,0:T(8,128)(2,1)S(1)} collective-permute-done((bf16[80,1024]{1,0:T(8,128)(2,1)S(1)}, bf16[80,1024]{1,0:T(8,128)(2,1)S(1)}, u32[]{:S(2)}, u32[]{:S(2)}) %collective-permute-start.1) | collective-permute-done | bytes 163872 | tf_op jit(solution)/shard_map/ppermute | solution.py:298
  403.2 0.0 collective-permute-start.8
  403.2 1.4 collective-permute-done.8.far
  404.6 0.7 place.9
  (5 shorter events, 0.0 us)
Async XLA Ops:
  318.1 44.4 %collective-permute-start.4 = (bf16[704,1024]{1,0:T(8,128)(2,1)}, bf16[704,1024]{1,0:T(8,128)(2,1)S(1)}, u32[]{:S(2)}, u32[]{:S(2)}) collective-permute-start(bf16[704,1024]{1,0:T(8,128)(2,1)} %get-tuple-element.59), channel_id=1, source_target_pairs={{0,2},{1,3},{2,0},{3,1},{4,6},{5,7},{6,4},{7,5}} | collective-permute-start | bytes 4325384 | tf_op jit(solution)/shard_map/ppermute | solution.py:298
  319.6 41.9 %collective-permute-start = (bf16[64,2816]{1,0:T(8,128)(2,1)}, bf16[64,2816]{1,0:T(8,128)(2,1)S(1)}, u32[]{:S(2)}, u32[]{:S(2)}) collective-permute-start(bf16[64,2816]{1,0:T(8,128)(2,1)} %get-tuple-element.52.near), channel_id=1, source_target_pairs={{0,1},{1,0},{2,3},{3,2},{4,5},{5,4},{6,7},{7,6}} | collective-permute-start | bytes 1081352 | tf_op jit(solution)/shard_map/ppermute | solution.py:299
  319.6 2.6 copy-start
  322.2 2.6 copy-start.1
  324.9 36.7 %copy-start.2 = (bf16[64,2816]{1,0:T(8,128)(2,1)S(1)}, bf16[64,2816]{1,0:T(8,128)(2,1)}, u32[]{:S(2)}) copy-start(bf16[64,2816]{1,0:T(8,128)(2,1)} %get-tuple-element.52.near) | copy-start | bytes 1081348
  361.6 1.5 copy-start.3
  362.5 3.4 collective-permute-start.5
  363.0 24.2 %copy-start.4 = (bf16[144,1024]{1,0:T(8,128)(2,1)S(1)}, bf16[144,1024]{1,0:T(8,128)(2,1)}, u32[]{:S(2)}) copy-start(bf16[144,1024]{1,0:T(8,128)(2,1)} %get-tuple-element.57) | copy-start | bytes 884740
  363.0 24.2 %collective-permute-start.3 = (bf16[480,1024]{1,0:T(8,128)(2,1)S(1)}, bf16[480,1024]{1,0:T(8,128)(2,1)S(1)}, u32[]{:S(2)}, u32[]{:S(2)}) collective-permute-start(bf16[480,1024]{1,0:T(8,128)(2,1)S(1)} %copy-done.3), channel_id=1, source_target_pairs={{0,2},{1,3},{2,0},{3,1},{4,6},{5,7},{6,4},{7,5}} | collective-permute-start | bytes 2949128 | tf_op jit(solution)/shard_map/ppermute | solution.py:298
  387.2 2.6 collective-permute-start.6
  387.2 9.4 %copy-start.5 = (bf16[80,1024]{1,0:T(8,128)(2,1)S(1)}, bf16[80,1024]{1,0:T(8,128)(2,1)}, u32[]{:S(2)}) copy-start(bf16[80,1024]{1,0:T(8,128)(2,1)} %get-tuple-element.56) | copy-start | bytes 491524
  387.2 9.4 %collective-permute-start.2 = (bf16[144,1024]{1,0:T(8,128)(2,1)S(1)}, bf16[144,1024]{1,0:T(8,128)(2,1)S(1)}, u32[]{:S(2)}, u32[]{:S(2)}) collective-permute-start(bf16[144,1024]{1,0:T(8,128)(2,1)S(1)} %copy-done.4), channel_id=1, source_target_pairs={{0,2},{1,3},{2,0},{3,1},{4,6},{5,7},{6,4},{7,5}} | collective-permute-start | bytes 884744 | tf_op jit(solution)/shard_map/ppermute | solution.py:298
  396.6 1.6 collective-permute-start.7
  396.6 6.6 %collective-permute-start.1 = (bf16[80,1024]{1,0:T(8,128)(2,1)S(1)}, bf16[80,1024]{1,0:T(8,128)(2,1)S(1)}, u32[]{:S(2)}, u32[]{:S(2)}) collective-permute-start(bf16[80,1024]{1,0:T(8,128)(2,1)S(1)} %copy-done.5), channel_id=1, source_target_pairs={{0,2},{1,3},{2,0},{3,1},{4,6},{5,7},{6,4},{7,5}} | collective-permute-start | bytes 491528 | tf_op jit(solution)/shard_map/ppermute | solution.py:298
  403.2 1.4 collective-permute-start.8
